TPU v7x, 32 devices: a whole 2x2x4 slice. The times are simulated.
32 devices in a mesh: blk: 8 (over z, x), rep: 4 (over y, core).
Axes of the slice: x: 2, y: 2, z: 4, core: 2. Of those that a mesh axis runs over, the one named last changes fastest.
Arguments:
- embeddings: float32 [16384, 768], P(('blk', 'rep')), may hold values from -6 to 6
- ranks: int32 [16384], replicated, may hold values from 0 to 16383, each once
Outputs:
- earlier_best: float32 [16384], P(('blk', 'rep'))
- later_best: float32 [16384], P(('blk', 'rep'))
Inputs may be any that keep to these rules, and one draw needn't show every extreme that they name: ranks is a permutation of 0 .. 16383.
All inputs are finite; a program needn't handle non-finite values.
Results may differ from a plain program's by a relative error of at most 0.0012.
Values may be sent and summed in bfloat16 or wider, within the bound.
A program may use at most 64 MiB of HBM per device.

v0:
```python
import functools

import jax
import jax.numpy as jnp
from jax import lax
from jax.experimental import pallas as pl
from jax.experimental.pallas import tpu as pltpu
from jax.sharding import PartitionSpec as P

STEPS = 3
CHUNKS = 4
MESH = pl.DeviceIdType.MESH


def kernel(
    blocks, copies, emb_ref, ranks_ref, early_ref, late_ref,
    host, visit, host_rank, visit_rank, row_acc, col_acc, col_in, row_out, row_in,
    z_send, x_send, y_send, core_send, two_send, one_send, relay_send, col_send, row_send,
    visit_recv, y_recv, core_recv, relay_recv, col_recv, row_recv,
):
    rows = emb_ref.shape[0]
    part = rows // CHUNKS
    b = lax.axis_index("blk")
    r = lax.axis_index("rep")
    odd = lax.rem(b, 2)
    even = odd == 0

    def blk(offset):
        return lax.rem(b + offset + blocks, blocks)

    core = r + 1 - 2 * lax.rem(r, 2)
    far = lax.rem(r + copies // 2, copies)
    far_core = lax.rem(core + copies // 2, copies)
    peers = (core, far, far_core)

    barrier = pltpu.get_barrier_semaphore()
    for offset in (1, 2, 3, -1, -2, -3):
        pl.semaphore_signal(barrier, inc=1, device_id=(blk(offset), r), device_id_type=MESH)
    for peer in peers:
        pl.semaphore_signal(barrier, inc=1, device_id=(b, peer), device_id_type=MESH)

    def normalise(i, _):
        at = pl.ds(pl.multiple_of(i * 64, 64), 64)
        x = emb_ref[at, :]
        squares = jnp.sum(x * x, axis=1, keepdims=True)
        host[0, at, :] = (x * lax.rsqrt(squares + 1e-06)).astype(jnp.bfloat16)
        return 0

    lax.fori_loop(0, rows // 64, normalise, 0)

    def cut(i):
        return pl.ds(pl.multiple_of(i * part, part), part)

    pl.semaphore_wait(barrier, 9)

    def send(src, dst, send_sem, recv_sem, device):
        copy = pltpu.make_async_remote_copy(
            src_ref=src, dst_ref=dst, send_sem=send_sem, recv_sem=recv_sem,
            device_id=device, device_id_type=MESH,
        )
        return copy

    def z_copy(i):
        return send(host.at[0, cut(i)], visit.at[1, cut(i)], z_send.at[i],
                    visit_recv.at[1, i], (blk(2), r))

    def x_copy(i):
        return send(host.at[0, cut(i)], visit.at[0, cut(i)], x_send.at[i],
                    visit_recv.at[0, i], (blk(1), r))

    def y_copy(i):
        return send(host.at[0, cut(i)], host.at[2, cut(i)], y_send.at[i],
                    y_recv.at[i], (b, far))

    def core_copy():
        return send(host.at[0], host.at[1], core_send, core_recv, (b, core))

    def relay_copy(i):
        return send(host.at[2, cut(i)], host.at[3, cut(i)], relay_send.at[i],
                    relay_recv.at[i], (b, core))

    def two_copy(i):
        slot = 2 - 2 * odd
        return send(visit.at[1, cut(i)], visit.at[slot, cut(i)], two_send.at[i],
                    visit_recv.at[slot, i], (blk(1 - 2 * odd), r))

    def one_copy(i):
        return send(visit.at[0, cut(i)], visit.at[2, cut(i)], one_send.at[i],
                    visit_recv.at[2, i], (blk(2), r))

    core_copy().start()
    for i in range(CHUNKS):
        z_copy(i).start()
        y_copy(i).start()

        @pl.when(even)
        def _():
            x_copy(i).start()

    owners = (r,) + peers
    for h, owner in enumerate(owners):
        line = ranks_ref[pl.ds(b * copies + owner, 1), :]
        host_rank[h] = jnp.broadcast_to(line, (128, rows)).T
    for slot, offset in enumerate((1, 2, 3, 0)):
        line = ranks_ref[pl.ds(blk(-offset) * copies + r, 1), :]
        visit_rank[slot] = jnp.broadcast_to(line, (8, rows))
    row_acc[...] = jnp.full(row_acc.shape, -1.0, jnp.float32)
    col_acc[...] = jnp.full(col_acc.shape, -1.0, jnp.float32)

    def score(other, slot, start, size, h):
        at = pl.ds(pl.multiple_of(start, size), size)
        scores = lax.dot_general(
            host[h], other[at, :], (((1,), (1,)), ((), ())),
            preferred_element_type=jnp.float32,
        )
        line = visit_rank[slot, 0:1, at]
        best = row_acc[h]
        for g in range(size // 128):
            kept = jnp.where(
                line[:, g * 128:(g + 1) * 128] < host_rank[h],
                scores[:, g * 128:(g + 1) * 128], jnp.float32(-1.0),
            )
            best = jnp.maximum(best, kept)
            column = jnp.max(kept.reshape(rows // 8, 8, 128), axis=0)
            there = pl.ds(pl.multiple_of(start + g * 128, 128), 128)
            col_acc[slot, :, there] = jnp.maximum(col_acc[slot, :, there], column)
        row_acc[h] = best

    wide = 256

    def sweep(other, slot, low, high):
        def step(t, _):
            h = low + t // (rows // wide)
            c = lax.rem(t, rows // wide)
            score(other, slot, c * wide, wide, h)
            return 0
        lax.fori_loop(0, (high - low) * (rows // wide), step, 0)

    sweep(host.at[0], 3, 0, 1)
    core_copy().wait_recv()
    sweep(host.at[0], 3, 1, 2)

    def arrive(i, _):
        y_copy(i).wait_recv()
        relay_copy(i).start()
        z_copy(i).wait_recv()
        two_copy(i).start()
        lax.fori_loop(0, 2, lambda h, c: (score(visit.at[1], 1, i * part, part, h), c)[1], 0)
        x_copy(i).wait_recv()

        @pl.when(even)
        def _():
            one_copy(i).start()

        lax.fori_loop(0, 2, lambda h, c: (score(visit.at[0], 0, i * part, part, h), c)[1], 0)
        return 0

    lax.fori_loop(0, CHUNKS, arrive, 0)
    for i in range(CHUNKS):
        relay_copy(i).wait_recv()
    sweep(host.at[0], 3, 2, 4)
    sweep(visit.at[1], 1, 2, 4)
    sweep(visit.at[0], 0, 2, 4)

    def col_copy(k):
        return send(col_acc.at[k], col_in.at[k], col_send.at[k], col_recv.at[k],
                    (blk(-1 - k), r))

    def last(i, _):
        one_copy(i).wait_recv()
        lax.fori_loop(0, 4, lambda h, c: (score(visit.at[2], 2, i * part, part, h), c)[1], 0)
        return 0

    col_copy(1).start()
    col_copy(0).start()
    lax.fori_loop(0, CHUNKS, last, 0)
    col_copy(2).start()

    def row_copy(k):
        return send(row_out.at[k], row_in.at[k], row_send.at[k], row_recv.at[k], (b, peers[k]))

    for k in range(3):
        best = jnp.max(row_acc[k + 1].T.reshape(16, 8, rows), axis=0)
        row_out[k] = best
        row_copy(k).start()

    early = jnp.max(row_acc[0].T.reshape(16, 8, rows), axis=0)
    late = col_acc[3]
    for k in range(3):
        row_copy(k).wait_recv()
        early = jnp.maximum(early, row_in[k])
    for k in range(3):
        col_copy(k).wait_recv()
        late = jnp.maximum(late, col_in[k])
    early_ref[...] = jnp.max(early, axis=0, keepdims=True)
    late_ref[...] = jnp.max(late, axis=0, keepdims=True)

    core_copy().wait_send()

    def drain(i, _):
        z_copy(i).wait_send()
        y_copy(i).wait_send()
        relay_copy(i).wait_send()
        two_copy(i).wait_send()

        @pl.when(even)
        def _():
            x_copy(i).wait_send()
            one_copy(i).wait_send()
        return 0

    lax.fori_loop(0, CHUNKS, drain, 0)
    for k in range(3):
        col_copy(k).wait_send()
        row_copy(k).wait_send()


def shards(embeddings, ranks):
    rows, width = embeddings.shape
    copies = lax.axis_size("rep")
    blocks = lax.axis_size("blk")
    lines = ranks.reshape(-1, rows)
    dma = pltpu.SemaphoreType.DMA
    vmem = pl.BlockSpec(memory_space=pltpu.VMEM)
    early, late = pl.pallas_call(
        functools.partial(kernel, blocks, copies),
        out_shape=[jax.ShapeDtypeStruct((1, rows), jnp.float32)] * 2,
        in_specs=[vmem, vmem],
        out_specs=[vmem, vmem],
        scratch_shapes=[
            pltpu.VMEM((4, rows, width), jnp.bfloat16),
            pltpu.VMEM((STEPS, rows, width), jnp.bfloat16),
            pltpu.VMEM((4, rows, 128), jnp.int32),
            pltpu.VMEM((4, 8, rows), jnp.int32),
            pltpu.VMEM((4, rows, 128), jnp.float32),
            pltpu.VMEM((4, 8, rows), jnp.float32),
            pltpu.VMEM((3, 8, rows), jnp.float32),
            pltpu.VMEM((3, 8, rows), jnp.float32),
            pltpu.VMEM((3, 8, rows), jnp.float32),
            dma((CHUNKS,)), dma((CHUNKS,)), dma((CHUNKS,)), dma,
            dma((CHUNKS,)), dma((CHUNKS,)), dma((CHUNKS,)), dma((3,)), dma((3,)),
            dma((STEPS, CHUNKS)), dma((CHUNKS,)), dma, dma((CHUNKS,)), dma((3,)), dma((3,)),
        ],
        compiler_params=pltpu.CompilerParams(
            collective_id=0, has_side_effects=True, vmem_limit_bytes=32 * 1024 * 1024
        ),
    )(embeddings, lines)
    return early.reshape(rows), late.reshape(rows)


def solution(mesh):
    return jax.shard_map(
        shards,
        mesh=mesh,
        in_specs=(P(("blk", "rep"), None), P()),
        out_specs=(P(("blk", "rep")), P(("blk", "rep"))),
        check_vma=False,
    )
```

profile of v0, /device:TPU:0, one launch (start us, length us, event | category | flops | bytes accessed | tf_op | source)
XLA Modules:
  0.0 50.7 jit_solution(17630896444168677964)
XLA Ops:
  0.6 0.9 %reshape.13.ranks_ref = s32[32,512]{1,0:T(8,128)S(1)} reshape(s32[16384]{0:T(1024)} %param.3) | data formatting | bytes 131072 | tf_op jit(solution)/shard_map/reshape | solution.py:222
  1.5 0.0 copy-start
  1.5 1.4 %copy-done = f32[512,768]{1,0:T(8,128)S(1)} copy-done((f32[512,768]{1,0:T(8,128)S(1)}, f32[512,768]{1,0:T(8,128)}, u32[]{:S(2)}) %copy-start) | copy-done | bytes 1572888
  2.9 46.7 %shard_map.41 = (f32[1,512]{1,0:T(1,128)S(1)}, f32[1,512]{1,0:T(1,128)S(1)}) custom-call(f32[512,768]{1,0:T(8,128)S(1)} %copy-done, s32[32,512]{1,0:T(8,128)S(1)} %reshape.13.ranks_ref), custom_call_target="tpu_custom_call" | custom-call | tf_op jit(solution)/shard_map/pallas_call | solution.py:225
  49.6 0.6 %copy.6 = f32[512]{0:T(512)} copy(f32[512]{0:T(512)S(1)} %bitcast.3) | data formatting | bytes 4096
  50.1 0.6 %copy.7 = f32[512]{0:T(512)} copy(f32[512]{0:T(512)S(1)} %bitcast.2) | data formatting | bytes 4096
Async XLA Ops:
  1.5 1.4 %copy-start = (f32[512,768]{1,0:T(8,128)S(1)}, f32[512,768]{1,0:T(8,128)}, u32[]{:S(2)}) copy-start(f32[512,768]{1,0:T(8,128)} %emb_ref.1) | copy-start | bytes 4718596
where the time goes:
time: 50.9 us; the launch traced here: 50.7 us
  Pallas kernels  46.7 us (92%)
  local copies, waits for them, and re-layouts  3.41 us (7%)
  between operations  0.65 us (1%)
    pallas_call x1, Pallas kernels, shards(): pl.pallas_call(functools.partial(kernel, blocks, copies), out_shape=[jax....  46.7 us
    unnamed x4, local copies, waits for them, and re-layouts  2.56 us

commit v1 on v0

v1 whole, which is shorter than its diff:
```python
import functools

import jax
import jax.numpy as jnp
from jax import lax
from jax.experimental import pallas as pl
from jax.experimental.pallas import tpu as pltpu
from jax.sharding import PartitionSpec as P

CHUNKS = 8
LANES = 128
MESH = pl.DeviceIdType.MESH


def kernel(
    blocks, copies, emb_hbm, ranks_hbm, early_ref, late_ref,
    emb, rank, host, vis, two,
    own_rank, vis_rank, two_rank,
    own_acc, vis_acc, two_acc, host_acc, swap_acc,
    row_out, row_in, back_out, back_in, two_out, two_in,
    emb_sem, rank_sem,
    core_send, core_recv, x_send, x_recv, y_send, y_recv, z_send, z_recv,
    relay_send, diag_send, diag_recv, twin_send, twin_recv, two_send, two_recv,
    row_send, row_sem, back_send, back_recv, twob_send, twob_recv,
):
    rows = emb.shape[0]
    part = rows // CHUNKS
    unit = rows // 2
    half = CHUNKS // 2
    lines = rows // LANES
    layers = blocks // 2
    wrap = layers == 4

    b = lax.axis_index("blk")
    r = lax.axis_index("rep")
    x = lax.rem(b, 2)
    l = b // 2
    other_x = 1 - x

    def flip_rep(k):
        dy, dc = k // 2, k % 2
        y, c = r // 2, lax.rem(r, 2)
        return 2 * (y + dy - 2 * y * dy) + c + dc - 2 * c * dc

    def flip_x(d):
        return x + d - 2 * x * d

    def peer(h):
        return (2 * l + flip_x(h // 4), flip_rep(h % 4))

    def layer(offset):
        return lax.rem(l + offset + layers, layers)

    if wrap:
        last = l // (layers - 1)
        is_relay = l == 1
        has_two = lax.rem(l, 2) == 0
    else:
        last = 0 * l
        is_relay = None
        has_two = None

    def if_relay(f):
        if wrap:
            pl.when(is_relay)(f)

    def if_two(f):
        if wrap:
            pl.when(has_two)(f)
        else:
            f()

    up = (2 * lax.rem(l + 1 + last, layers) + x, r)
    down = (2 * layer(-1) + x, r)
    far_up = (2 * layer(2) + x, r)
    far_down = (2 * layer(-2) + x, r)

    def cut(i):
        return pl.ds(pl.multiple_of(i * part, part), part)

    def emb_copy(i):
        return pltpu.make_async_copy(emb_hbm.at[cut(i)], emb.at[cut(i)], emb_sem.at[i])

    def rank_copy(k):
        size = 2 * copies * lines
        return pltpu.make_async_copy(
            ranks_hbm.at[pl.ds(pl.multiple_of(layer(-k) * size, size), size)], rank.at[k], rank_sem.at[k]
        )

    for i in range(CHUNKS):
        emb_copy(i).start()
    for k in range(3):
        rank_copy(k).start()

    barrier = pltpu.get_barrier_semaphore()
    greet = [peer(h) for h in range(1, 8)]
    for offset in (1, -1):
        greet.append((2 * layer(offset) + x, r))
    for offset in ((2,) if wrap else (2, -2)):
        greet.append((2 * layer(offset) + x, r))
        greet.append((2 * layer(offset) + other_x, r))
    for device in greet:
        pl.semaphore_signal(barrier, inc=1, device_id=device, device_id_type=MESH)

    def send(src, dst, send_sem, recv_sem, device):
        return pltpu.make_async_remote_copy(
            src_ref=src, dst_ref=dst, send_sem=send_sem, recv_sem=recv_sem,
            device_id=device, device_id_type=MESH,
        )

    def core_copy(i):
        return send(host.at[0, cut(i)], host.at[1, cut(i)], core_send.at[i], core_recv.at[i], peer(1))

    def x_copy(i):
        return send(host.at[0, cut(i)], host.at[4, cut(i)], x_send.at[i], x_recv.at[i], peer(4))

    def y_copy(i):
        return send(host.at[0, cut(i)], host.at[2, cut(i)], y_send.at[i], y_recv.at[i], peer(2))

    def z_copy(i):
        return send(host.at[0, cut(i)], vis.at[last, cut(i)], z_send.at[i], z_recv.at[last, i], up)

    def z_wait(slot, i):
        send(host.at[0, cut(i)], vis.at[slot, cut(i)], z_send.at[i], z_recv.at[slot, i], up).wait_recv()

    def relay_copy(i):
        return send(vis.at[1, cut(i)], vis.at[0, cut(i)], relay_send.at[i], z_recv.at[0, i], down)

    def diag_copy(i, by_x):
        src, device = (host.at[2, cut(i)], peer(4)) if by_x else (host.at[4, cut(i)], peer(2))
        return send(src, host.at[6, cut(i)], diag_send.at[i], diag_recv.at[i], device)

    def twin_copy(k, i):
        slot = 2 + 2 * k
        return send(host.at[slot, cut(i)], host.at[slot + 1, cut(i)], twin_send.at[k, i], twin_recv.at[k, i], peer(1))

    def two_copy(i):
        at = pl.ds(pl.multiple_of(x * unit + i * part, part), part)
        return send(host.at[4 * other_x, at], two.at[cut(i)], two_send.at[i], two_recv.at[i], far_up)

    def normalise(i):
        emb_copy(i).wait()
        v = emb[cut(i), :]
        squares = jnp.sum(v * v, axis=1, keepdims=True)
        host[0, cut(i), :] = (v * lax.rsqrt(squares + 1e-06)).astype(jnp.bfloat16)

    def launch(i):
        core_copy(i).start()
        x_copy(i).start()
        y_copy(i).start()
        z_copy(i).start()

    normalise(0)
    normalise(1)
    pl.semaphore_wait(barrier, len(greet))

    def prepare(i, _):
        launch(i - 2)
        normalise(i)
        return 0

    lax.fori_loop(2, CHUNKS, prepare, 0)

    for k in range(3):
        rank_copy(k).wait()
    launch(CHUNKS - 2)
    launch(CHUNKS - 1)

    sign = 2 * x - 1

    def spread(slot, row, count, out, factor=None):
        for g in range(count):
            line = rank[slot, pl.ds(row + g, 1), :]
            if factor is not None:
                line = line * factor
            out[g * LANES:(g + 1) * LANES, :] = jnp.broadcast_to(line, (LANES, LANES)).T

    mine = (copies * x + r) * lines
    spread(0, mine, lines, own_rank)
    own_acc[...] = jnp.full(own_acc.shape, -1.0, jnp.float32)
    vis_acc[...] = jnp.full(vis_acc.shape, -1.0, jnp.float32)
    two_acc[...] = jnp.full(two_acc.shape, -1.0, jnp.float32)
    host_acc[...] = jnp.full(host_acc.shape, -1.0, jnp.float32)
    swap_acc[...] = jnp.full(swap_acc.shape, -1.0, jnp.float32)

    def score(guest, guest_rank, guest_acc, h, u, acc, slot, factor=None):
        at = pl.ds(pl.multiple_of(u * unit, unit), unit)
        scores = lax.dot_general(
            guest[...], host[h, at, :], (((1,), (1,)), ((), ())), preferred_element_type=jnp.float32
        )
        row = (copies * flip_x(h // 4) + flip_rep(h % 4)) * lines + u * (unit // LANES)
        best = guest_acc[...]
        for g in range(unit // LANES):
            line = rank[0, pl.ds(row + g, 1), :]
            if factor is not None:
                line = line * factor
            kept = jnp.where(
                guest_rank[...] < line, scores[:, g * LANES:(g + 1) * LANES], jnp.float32(-1.0)
            )
            best = jnp.maximum(best, kept)
            column = jnp.max(kept.reshape(kept.shape[0] // 8, 8, LANES), axis=0)
            there = pl.ds(pl.multiple_of(u * unit + g * LANES, LANES), LANES)
            acc[slot, :, there] = jnp.maximum(acc[slot, :, there], column)
        guest_acc[...] = best

    def own_score(h, u):
        score(host.at[0], own_rank, own_acc, h, u, host_acc, h)

    def vis_score(h, u):
        score(vis.at[0], vis_rank.at[0], vis_acc.at[0], h, u, host_acc, h)

    def swap_score(h, u):
        score(vis.at[1], vis_rank.at[1], vis_acc.at[1], h, u, swap_acc, h - 4, sign)

    def two_score(h, u):
        score(two, two_rank, two_acc, h, u, host_acc, h)

    def sweep(f, low, high, first=0, count=2):
        def body(t, _):
            f(low + t // count, first + lax.rem(t, count))
            return 0
        lax.fori_loop(0, (high - low) * count, body, 0)

    sweep(own_score, 0, 1)
    spread(1, mine, lines, vis_rank.at[0])
    spread(2, mine, lines, vis_rank.at[1], sign)
    spread(2, (copies + r) * lines + x * (lines // 2), lines // 2, two_rank)

    def core_wait(i, _):
        core_copy(i).wait_recv()
        return 0

    lax.fori_loop(0, CHUNKS, core_wait, 0)
    sweep(own_score, 1, 2)

    def arrive(p, _):
        for by_x in (True, False):
            i = 2 * p + (0 if by_x else 1)
            y_copy(i).wait_recv()
            twin_copy(0, i).start()
            x_copy(i).wait_recv()
            twin_copy(1, i).start()
            diag_copy(i, by_x).start()

            @if_relay
            def _():
                z_wait(1, i)
                relay_copy(i).start()
        return 0

    def twins(k, first):
        def body(i, _):
            twin_copy(k, i).wait_recv()
            return 0
        lax.fori_loop(first, first + half, body, 0)

    for u in range(2):
        lax.fori_loop(u * (half // 2), (u + 1) * (half // 2), arrive, 0)
        if u == 1:
            @if_two
            def _():
                for i in range(half):
                    two_copy(i).start()
        twins(0, u * half)
        twins(1, u * half)
        sweep(own_score, 2, 4, u, 1)

        @pl.when(x == 0)
        def _():
            sweep(own_score, 4, 6, u, 1)

    def z_arrive(i, _):
        z_wait(0, i)
        return 0

    lax.fori_loop(0, CHUNKS, z_arrive, 0)
    sweep(vis_score, 0, 6)

    @if_relay
    def _():
        sweep(swap_score, 4, 6)

    def lanes(acc):
        return jnp.max(acc[...].T, axis=0, keepdims=True)

    def back_copy(slot):
        device = far_down if slot else (2 * lax.rem(l + layers - 1, layers) + x, r)
        return send(back_out.at[slot], back_in.at[slot], back_send.at[slot], back_recv.at[slot], device)

    def diag_arrive(i, _):
        diag_copy(i, True).wait_recv()
        twin_copy(2, i).start()
        return 0

    none = jnp.full((1, rows), -1.0, jnp.float32)
    for u in range(2):
        lax.fori_loop(u * half, (u + 1) * half, diag_arrive, 0)
        twins(2, u * half)
        sweep(vis_score, 6, 8, u, 1)
        if u == 1:
            back_out[0, 0:1, :] = none
            back_out[0, 1:2, :] = lanes(vis_acc.at[0])
            back_copy(0).start()

        @pl.when(x == 0)
        def _():
            sweep(own_score, 6, 8, u, 1)

        @if_relay
        def _():
            sweep(swap_score, 6, 8, u, 1)

    @if_relay
    def _():
        best = lanes(vis_acc.at[1])
        back_out[1, 0:1, :] = jnp.where(x == 0, best, none)
        back_out[1, 1:2, :] = jnp.where(x == 0, none, best)
        back_copy(1).start()

    @if_two
    def _():
        def two_arrive(i, _):
            two_copy(i).wait_recv()
            return 0
        lax.fori_loop(0, half, two_arrive, 0)

        def body(t, _):
            two_score(4 * x + t // 2, lax.rem(t, 2))
            return 0
        lax.fori_loop(0, 8, body, 0)

    def row_copy(h):
        return send(row_out.at[h - 1], row_in.at[h - 1], row_send.at[h - 1], row_sem.at[h - 1], peer(h))

    for h in range(7, 0, -1):
        best = jnp.max(host_acc[h], axis=0, keepdims=True)
        late = none
        if h >= 4 and wrap:
            swapped = jnp.max(swap_acc[h - 4], axis=0, keepdims=True)
            late = jnp.where(x == 0, swapped, none)
            best = jnp.where(x == 0, best, jnp.maximum(best, swapped))
        row_out[h - 1, 0:1, :] = best
        row_out[h - 1, 1:2, :] = late
        row_copy(h).start()

    def twob_copy(k):
        return send(two_out, two_in.at[k], twob_send, twob_recv.at[k], (2 * layer(-2) + 1, r))

    @if_two
    def _():
        two_out[...] = jnp.broadcast_to(lanes(two_acc), two_out.shape)
        twob_copy(x).start()

    early = jnp.max(host_acc[0], axis=0, keepdims=True)
    late = lanes(own_acc)
    early_ref[...] = early
    late_ref[...] = late

    def take(pair):
        early_ref[...] = jnp.maximum(early_ref[...], pair[0:1, :])
        late_ref[...] = jnp.maximum(late_ref[...], pair[1:2, :])

    for h in range(1, 8):
        row_copy(h).wait_recv()
        take(row_in.at[h - 1])
    back_copy(0).wait_recv()
    take(back_in.at[0])

    @if_two
    def _():
        @pl.when(x == 1)
        def _():
            for k in range(2):
                twob_copy(k).wait_recv()
                at = slice(k * unit, (k + 1) * unit)
                late_ref[:, at] = jnp.maximum(late_ref[:, at], two_in[k, 0:1, :])

    if wrap:
        @pl.when(l == layers - 1)
        def _():
            back_copy(1).wait_recv()
            take(back_in.at[1])

    def drain(i, _):
        core_copy(i).wait_send()
        x_copy(i).wait_send()
        y_copy(i).wait_send()
        z_copy(i).wait_send()
        diag_copy(i, True).wait_send()
        for k in range(3):
            twin_copy(k, i).wait_send()

        @if_relay
        def _():
            relay_copy(i).wait_send()
        return 0

    lax.fori_loop(0, CHUNKS, drain, 0)

    @if_two
    def _():
        for i in range(half):
            two_copy(i).wait_send()
        twob_copy(0).wait_send()

    for h in range(1, 8):
        row_copy(h).wait_send()
    back_copy(0).wait_send()

    @if_relay
    def _():
        back_copy(1).wait_send()


def shards(embeddings, ranks):
    rows, width = embeddings.shape
    copies = lax.axis_size("rep")
    blocks = lax.axis_size("blk")
    lines = rows // LANES
    dma = pltpu.SemaphoreType.DMA
    vmem = pl.BlockSpec(memory_space=pltpu.VMEM)
    hbm = pl.BlockSpec(memory_space=pltpu.HBM)
    f32, i32, bf16 = jnp.float32, jnp.int32, jnp.bfloat16
    half = CHUNKS // 2
    early, late = pl.pallas_call(
        functools.partial(kernel, blocks, copies),
        out_shape=[jax.ShapeDtypeStruct((1, rows), f32)] * 2,
        in_specs=[hbm, hbm],
        out_specs=[vmem, vmem],
        scratch_shapes=[
            pltpu.VMEM((rows, width), f32),
            pltpu.VMEM((3, 2 * copies * lines, LANES), i32),
            pltpu.VMEM((8, rows, width), bf16),
            pltpu.VMEM((2, rows, width), bf16),
            pltpu.VMEM((rows // 2, width), bf16),
            pltpu.VMEM((rows, LANES), i32),
            pltpu.VMEM((2, rows, LANES), i32),
            pltpu.VMEM((rows // 2, LANES), i32),
            pltpu.VMEM((rows, LANES), f32),
            pltpu.VMEM((2, rows, LANES), f32),
            pltpu.VMEM((rows // 2, LANES), f32),
            pltpu.VMEM((8, 8, rows), f32),
            pltpu.VMEM((4, 8, rows), f32),
            pltpu.VMEM((7, 2, rows), f32),
            pltpu.VMEM((7, 2, rows), f32),
            pltpu.VMEM((2, 2, rows), f32),
            pltpu.VMEM((2, 2, rows), f32),
            pltpu.VMEM((2, rows // 2), f32),
            pltpu.VMEM((2, 2, rows // 2), f32),
            dma((CHUNKS,)), dma((3,)),
            dma((CHUNKS,)), dma((CHUNKS,)), dma((CHUNKS,)), dma((CHUNKS,)),
            dma((CHUNKS,)), dma((CHUNKS,)), dma((CHUNKS,)), dma((2, CHUNKS)),
            dma((CHUNKS,)), dma((CHUNKS,)), dma((CHUNKS,)),
            dma((3, CHUNKS)), dma((3, CHUNKS)), dma((half,)), dma((half,)),
            dma((7,)), dma((7,)), dma((2,)), dma((2,)), dma, dma((2,)),
        ],
        compiler_params=pltpu.CompilerParams(
            collective_id=0, has_side_effects=True, vmem_limit_bytes=32 * 1024 * 1024
        ),
    )(embeddings, ranks.reshape(-1, LANES))
    return early.reshape(rows), late.reshape(rows)


def solution(mesh):
    return jax.shard_map(
        shards,
        mesh=mesh,
        in_specs=(P(("blk", "rep"), None), P()),
        out_specs=(P(("blk", "rep")), P(("blk", "rep"))),
        check_vma=False,
    )
```

time: 50.9 us -> 62.9 us (1.24)
  Pallas kernels: 46.7 us -> 58.7 us
    pallas_call x1, Pallas kernels: 46.7 us -> 58.7 us  [shards(): pl.pallas_call(functools.partial(kernel, blocks, copies), out_shape=[jax....]
    reshape x1 -> x0, local copies, waits for them, and re-layouts: 0.85 us -> none  [shards(): lines = ranks.reshape(-1, rows)]
    unnamed x4 -> x6, local copies, waits for them, and re-layouts: 2.56 us -> 3.4 us
where the time goes in v1:
time: 62.9 us; the launch traced here: 62.7 us
  Pallas kernels  58.7 us (93%)
  local copies, waits for them, and re-layouts  3.4 us (5%)
  between operations  0.65 us (1%)
    pallas_call x1, Pallas kernels, shards(): pl.pallas_call(functools.partial(kernel, blocks, copies), out_shape=[jax....  58.7 us
    unnamed x6, local copies, waits for them, and re-layouts  3.4 us

profile of v1, /device:TPU:0, one launch (start us, length us, event | category | flops | bytes accessed | tf_op | source)
XLA Modules:
  0.0 62.7 jit_solution(14397256238826477124)
XLA Ops:
  0.6 0.0 copy-start
  0.6 1.4 %copy-done = f32[512,768]{1,0:T(8,128)S(1)} copy-done((f32[512,768]{1,0:T(8,128)S(1)}, f32[512,768]{1,0:T(8,128)}, u32[]{:S(2)}) %copy-start) | copy-done | bytes 1572888
  2.0 0.0 copy-start.1
  2.0 0.8 %copy-done.1 = s32[16384]{0:T(1024)S(1)} copy-done((s32[16384]{0:T(1024)S(1)}, s32[16384]{0:T(1024)}, u32[]{:S(2)}) %copy-start.1) | copy-done | bytes 65560
  2.9 58.7 %shard_map.41 = (f32[1,512]{1,0:T(1,128)S(1)}, f32[1,512]{1,0:T(1,128)S(1)}) custom-call(f32[512,768]{1,0:T(8,128)S(1)} %copy-done, s32[128,128]{1,0:T(8,128)S(1)} %bitcast.3), custom_call_target="tpu_custom_call" | custom-call | tf_op jit(solution)/shard_map/pallas_call | solution.py:425
  61.6 0.6 copy.6
  62.2 0.6 copy.7
Async XLA Ops:
  0.6 1.4 %copy-start = (f32[512,768]{1,0:T(8,128)S(1)}, f32[512,768]{1,0:T(8,128)}, u32[]{:S(2)}) copy-start(f32[512,768]{1,0:T(8,128)} %emb_hbm.1) | copy-start | bytes 4718596
  2.0 0.8 %copy-start.1 = (s32[16384]{0:T(1024)S(1)}, s32[16384]{0:T(1024)}, u32[]{:S(2)}) copy-start(s32[16384]{0:T(1024)} %param.3) | copy-start | bytes 196612

commit v2 on v1

v2 whole, which is shorter than its diff:
```python
import functools

import jax
import jax.numpy as jnp
from jax import lax
from jax.experimental import pallas as pl
from jax.experimental.pallas import tpu as pltpu
from jax.sharding import PartitionSpec as P

CHUNKS = 8
LANES = 128
MESH = pl.DeviceIdType.MESH


def kernel(
    blocks, copies, emb_hbm, ranks_hbm, early_ref, late_ref,
    emb, rank, mem, pair, two,
    guest_rank, pair_rank, two_rank, guest_acc, pair_acc, two_acc, host_acc, swap_acc,
    row_out, row_in, back_out, back_in, two_out, two_in,
    emb_sem, rank_sem,
    core_send, core_recv, x_send, x_recv, y_send, y_recv, z_send, z_recv, pair_recv,
    relay_send, diag_send, diag_recv, twin_send, twin_recv, two_send, two_recv,
    row_send, row_sem, back_send, back_recv, twob_send, twob_recv,
):
    rows = emb.shape[0]
    part = rows // CHUNKS
    unit = rows // 2
    small = part // 2
    half = CHUNKS // 2
    lines = rows // LANES
    layers = blocks // 2
    wrap = layers == 4

    b = blocks - 1 - lax.axis_index("blk")
    r = lax.axis_index("rep")
    x = lax.rem(b, 2)
    l = b // 2

    def flip_rep(k):
        dy, dc = k // 2, k % 2
        y, c = r // 2, lax.rem(r, 2)
        return 2 * (y + dy - 2 * y * dy) + c + dc - 2 * c * dc

    def flip_x(d):
        return x + d - 2 * x * d

    def device(row, column, copy):
        return (blocks - 1 - 2 * row - column, copy)

    def peer(h):
        return device(l, flip_x(h // 4), flip_rep(h % 4))

    def layer(offset):
        return lax.rem(l + offset + layers, layers)

    if wrap:
        last = l // (layers - 1)
        is_relay = l == 1
        has_two = lax.rem(l, 2) == 0
    else:
        last = 0 * l
        is_relay = None
        has_two = None

    def if_relay(f):
        if wrap:
            pl.when(is_relay)(f)

    def unless_relay(f):
        if wrap:
            pl.when(l != 1)(f)
        else:
            f()

    def if_two(f):
        if wrap:
            pl.when(has_two)(f)
        else:
            f()

    up = device(layer(1), x, r)
    down = device(layer(-1), x, r)
    far_up = device(layer(2), x, r)
    far_down = device(layer(-2), x, r)

    def cut(i):
        return pl.ds(pl.multiple_of(i * part, part), part)

    def emb_copy(i):
        return pltpu.make_async_copy(emb_hbm.at[cut(i)], emb.at[cut(i)], emb_sem.at[i])

    def rank_copy(k):
        size = 2 * copies * lines
        return pltpu.make_async_copy(
            ranks_hbm.at[pl.ds(pl.multiple_of((layers - 1 - layer(-k)) * size, size), size)],
            rank.at[k], rank_sem,
        )

    barrier = pltpu.get_barrier_semaphore()

    def greet(target):
        pl.semaphore_signal(barrier, inc=1, device_id=target, device_id_type=MESH)

    for h in (1, 2, 4):
        greet(peer(h))
    if wrap:
        @pl.when(l == 0)
        def _():
            greet(device(l + 1, x, r))

        @pl.when(l > 0)
        def _():
            greet(down)

        @pl.when(l < layers - 1)
        def _():
            greet(far_up)
        expected = 5 - last
    else:
        greet(down)
        greet(far_down)
        expected = 5

    for i in range(CHUNKS):
        emb_copy(i).start()
    for k in range(3):
        rank_copy(k).start()

    def send(src, dst, send_sem, recv_sem, device):
        return pltpu.make_async_remote_copy(
            src_ref=src, dst_ref=dst, send_sem=send_sem, recv_sem=recv_sem,
            device_id=device, device_id_type=MESH,
        )

    def host(h):
        return mem.at[h + 1]

    def area(u):
        return pl.ds(u * unit, unit)

    every = pl.ds(0, rows)

    def core_copy(at):
        return send(host(0).at[at], host(1).at[at], core_send, core_recv, peer(1))

    def x_copy(i, at=None):
        at = cut(i) if at is None else at
        return send(host(0).at[at], host(4).at[at], x_send, x_recv.at[i], peer(4))

    def y_copy(i, at=None):
        at = cut(i) if at is None else at
        return send(host(0).at[at], host(2).at[at], y_send, y_recv.at[i], peer(2))

    def z_copy(u, at):
        return send(host(0).at[at], mem.at[0, at], z_send, z_recv.at[u], up)

    def far_copy(k, at):
        return send(host(0).at[at], pair.at[at], z_send, pair_recv.at[k], far_down)

    def relay_copy(u, at):
        return send(pair.at[at], mem.at[0, at], relay_send, z_recv.at[u], down)

    def diag_copy(i, by_x, at=None):
        at = cut(i) if at is None else at
        source, target = (2, peer(4)) if by_x else (4, peer(2))
        return send(host(source).at[at], host(6).at[at], diag_send, diag_recv.at[i], target)

    def twin_copy(k, u, at):
        slot = 2 + 2 * k
        return send(
            host(slot).at[at], host(slot + 1).at[at], twin_send.at[k], twin_recv.at[k, u], peer(1)
        )

    def two_copy(i, size):
        at = pl.ds(pl.multiple_of(x * unit + i * part, part), size)
        there = pl.ds(i * part, size)
        return send(host(4 * (1 - x)).at[at], two.at[there], two_send, two_recv, far_up)

    def normalise(i):
        emb_copy(i).wait()
        v = emb[cut(i), :]
        squares = jnp.sum(v * v, axis=1, keepdims=True)
        mem[1, cut(i), :] = (v * lax.rsqrt(squares + 1e-06)).astype(jnp.bfloat16)

    def piece(k):
        return pl.ds(pl.multiple_of(k * small, small), small)

    def ascend(i):
        def far():
            for n in range(part // small):
                k = i * (part // small) + n
                far_copy(k, piece(k)).start()

        if wrap:
            pl.when(last == 1)(far)

            @pl.when(last == 0)
            def _():
                z_copy(i // half, cut(i)).start()
        else:
            z_copy(i // half, cut(i)).start()

    def launch(i):
        ascend(i)
        x_copy(i).start()
        y_copy(i).start()
        core_copy(cut(i)).start()

    with jax.named_scope("norm"):
        normalise(0)
        normalise(1)
    with jax.named_scope("barrier"):
        pl.semaphore_wait(barrier, expected)

    def prepare(i, _):
        launch(i - 2)
        normalise(i)
        return 0

    with jax.named_scope("prepare"):
        launch(0)
        normalise(2)
        lax.fori_loop(3, CHUNKS, prepare, 0)
        for k in range(3):
            rank_copy(k).wait()
        launch(CHUNKS - 2)
        launch(CHUNKS - 1)

    def relay(i):
        for n in range(part // small):
            k = i * (part // small) + n
            with jax.named_scope("w"):
                far_copy(k, piece(k)).wait_recv()
            relay_copy(i // half, piece(k)).start()

    sign = 2 * x - 1

    def place(column, copy):
        return (copies * (1 - column) + copy) * lines

    def spread(slot, row, count, out, factor=None):
        for g in range(count):
            line = rank[slot, pl.ds(row + g, 1), :]
            if factor is not None:
                line = line * factor
            out[g * LANES:(g + 1) * LANES, :] = jnp.broadcast_to(line, (LANES, LANES)).T

    spread(0, place(x, r), lines, guest_rank.at[1])
    for acc in (guest_acc, pair_acc, two_acc, host_acc, swap_acc):
        acc[...] = jnp.full(acc.shape, -1.0, jnp.float32)

    def score(guest, guest_line, best_ref, h, u, acc, slot, factor=None, slots=1):
        if u is None:
            low, size = 0, rows
            hosts = mem[pl.ds(h + 1, slots)].reshape(slots * rows, mem.shape[2])
        else:
            low, size = u * unit, unit
            hosts = mem[h + 1, area(u), :]
        count = guest_line.size // LANES
        lhs = guest[...].reshape(count, hosts.shape[1])
        scores = lax.dot_general(
            lhs, hosts, (((1,), (1,)), ((), ())), preferred_element_type=jnp.float32
        )
        own = guest_line[...].reshape(count, LANES)
        best = best_ref[...].reshape(count, LANES)
        for k in range(slots):
            row = place(flip_x((h + k) // 4), flip_rep((h + k) % 4))
            for g in range(size // LANES):
                line = rank[0, pl.ds(row + low // LANES + g, 1), :]
                if factor is not None:
                    line = line * factor
                at = slice(k * size + g * LANES, k * size + (g + 1) * LANES)
                kept = jnp.where(line < own, scores[:, at], jnp.float32(-1.0))
                best = jnp.maximum(best, kept)
                column = jnp.max(kept.reshape(count // 8, 8, LANES), axis=0)
                there = slice(low + g * LANES, low + (g + 1) * LANES)
                acc[slot + k, :, there] = jnp.maximum(acc[slot + k, :, there], column)
        best_ref[...] = best.reshape(best_ref.shape)

    def own_score(h, u=None):
        score(mem.at[1], guest_rank.at[1], guest_acc.at[1], h, u, host_acc, h)

    def up_score(h, u=None):
        score(mem.at[0], guest_rank.at[0], guest_acc.at[0], h, u, host_acc, h)

    def both_score(h, u):
        score(mem.at[0:2], guest_rank, guest_acc, h, u, host_acc, h)

    def part_score(v, h, u=None):
        at = slice(v * unit, (v + 1) * unit)
        score(mem.at[0, at], guest_rank.at[0, at], guest_acc.at[0, at], h, u, host_acc, h)

    def pair_score(h):
        score(pair, pair_rank, pair_acc, h, None, swap_acc, h - 4, sign)

    def two_score(h):
        score(two, two_rank, two_acc, h, None, host_acc, h, slots=2)

    def sweep(f, low, high):
        def body(h, _):
            f(h)
            return 0
        lax.fori_loop(low, high, body, 0)

    def each(f, low, high):
        def body(i, _):
            f(i)
            return 0
        lax.fori_loop(low, high, body, 0)

    with jax.named_scope("own0"):
        own_score(0)
    spread(1, place(x, r), lines, guest_rank.at[0])
    spread(2, place(x, r), lines, pair_rank, sign)
    spread(2, place(1, r) + x * (lines // 2), lines // 2, two_rank)
    with jax.named_scope("core"):
        core_copy(every).wait_recv()
    with jax.named_scope("own1"):
        own_score(1)

    def arrive(p):
        for by_x in (True, False):
            i = 2 * p + (0 if by_x else 1)
            u = i // half

            @if_relay
            def _():
                relay(i)

            with jax.named_scope("y"):
                y_copy(i).wait_recv()
            twin_copy(0, u, cut(i)).start()
            with jax.named_scope("x"):
                x_copy(i).wait_recv()
            twin_copy(1, u, cut(i)).start()
            diag_copy(i, by_x).start()

    def z_wait(u):
        with jax.named_scope("z"):
            z_copy(u, area(u)).wait_recv()

    for u in range(2):
        each(arrive, u * (half // 2), (u + 1) * (half // 2))
        with jax.named_scope("twin"):
            for k in range(2):
                twin_copy(k, u, area(u)).wait_recv()

        @unless_relay
        def _():
            with jax.named_scope("own25"):
                sweep(lambda h: own_score(h, u), 2, 6 - 2 * x)
            if u == 0:
                z_wait(0)
                with jax.named_scope("v0"):
                    sweep(lambda h: part_score(0, h), 0, 2)
            else:
                with jax.named_scope("v0"):
                    sweep(lambda h: part_score(0, h), 2, 6)

                @if_two
                def _():
                    two_copy(0, unit).start()
                z_wait(1)
                with jax.named_scope("v1"):
                    sweep(lambda h: part_score(1, h), 0, 6)

    @if_relay
    def _():
        with jax.named_scope("own25"):
            sweep(own_score, 2, 6 - 2 * x)
        z_wait(0)
        z_wait(1)
        with jax.named_scope("v01"):
            sweep(up_score, 0, 6)

    def lanes(acc):
        return jnp.max(acc[...].T, axis=0, keepdims=True)

    none = jnp.full((1, rows), -1.0, jnp.float32)

    def back_copy(slot):
        target = far_up if slot else device(layer(-1), x, r)
        return send(back_out.at[slot], back_in.at[slot], back_send.at[slot], back_recv.at[slot], target)

    def diag_arrive(i):
        diag_copy(i, True).wait_recv()
        twin_copy(2, i // half, cut(i)).start()

    @if_relay
    def _():
        with jax.named_scope("p45"):
            sweep(pair_score, 4, 6)

    for u in range(2):
        with jax.named_scope("diag"):
            each(diag_arrive, u * half, (u + 1) * half)
            twin_copy(2, u, area(u)).wait_recv()
        with jax.named_scope("last"):
            @pl.when(x == 0)
            def _():
                sweep(lambda h: both_score(h, u), 6, 8)

            @pl.when(x == 1)
            def _():
                sweep(lambda h: up_score(h, u), 6, 8)

    back_out[0, 0:1, :] = none
    back_out[0, 1:2, :] = lanes(guest_acc.at[0])
    back_copy(0).start()

    @if_relay
    def _():
        with jax.named_scope("p67"):
            sweep(pair_score, 6, 8)
            best = lanes(pair_acc)
            back_out[1, 0:1, :] = jnp.where(x == 0, best, none)
            back_out[1, 1:2, :] = jnp.where(x == 0, none, best)
            back_copy(1).start()

    @if_two
    def _():
        with jax.named_scope("two"):
            two_copy(0, unit).wait_recv()
        with jax.named_scope("v2"):
            sweep(lambda k: two_score(4 * x + 2 * k), 0, 2)

    def row_copy(h):
        return send(row_out.at[h - 1], row_in.at[h - 1], row_send, row_sem, peer(h))

    with jax.named_scope("rows"):
        for h in range(7, 0, -1):
            best = jnp.max(host_acc[h], axis=0, keepdims=True)
            other = none
            if h >= 4 and wrap:
                swapped = jnp.max(swap_acc[h - 4], axis=0, keepdims=True)
                other = jnp.where(x == 0, swapped, none)
                best = jnp.where(x == 0, best, jnp.maximum(best, swapped))
            row_out[h - 1, 0:1, :] = best
            row_out[h - 1, 1:2, :] = other
            row_copy(h).start()

    def twob_copy(k):
        return send(two_out, two_in.at[k], twob_send, twob_recv, device(layer(-2), 1, r))

    @if_two
    def _():
        two_out[...] = jnp.broadcast_to(lanes(two_acc), two_out.shape)
        twob_copy(x).start()

    late_ref[...] = jnp.max(host_acc[0], axis=0, keepdims=True)
    early_ref[...] = lanes(guest_acc.at[1])

    def take(best):
        late_ref[...] = jnp.maximum(late_ref[...], best[0:1, :])
        early_ref[...] = jnp.maximum(early_ref[...], best[1:2, :])

    with jax.named_scope("rowin"):
        send(row_out, row_in, row_send, row_sem, peer(1)).wait_recv()
        for h in range(1, 8):
            take(row_in.at[h - 1])
    with jax.named_scope("back"):
        back_copy(0).wait_recv()
        take(back_in.at[0])

        @if_two
        def _():
            @pl.when(x == 1)
            def _():
                send(two_in, two_in, twob_send, twob_recv, far_up).wait_recv()
                for k in range(2):
                    at = slice(k * unit, (k + 1) * unit)
                    early_ref[:, at] = jnp.maximum(early_ref[:, at], two_in[k, 0:1, :])

        if wrap:
            @pl.when(last == 1)
            def _():
                back_copy(1).wait_recv()
                take(back_in.at[1])

    with jax.named_scope("drain"):
        core_copy(every).wait_send()
        x_copy(0, every).wait_send()
        y_copy(0, every).wait_send()
        z_copy(0, every).wait_send()
        diag_copy(0, True, every).wait_send()
        for k in range(3):
            twin_copy(k, 0, every).wait_send()

        @if_two
        def _():
            two_copy(0, unit).wait_send()
            twob_copy(0).wait_send()

        send(row_out, row_in, row_send, row_sem, peer(1)).wait_send()
        back_copy(0).wait_send()

        @if_relay
        def _():
            relay_copy(0, every).wait_send()
            back_copy(1).wait_send()


def shards(embeddings, ranks):
    rows, width = embeddings.shape
    copies = lax.axis_size("rep")
    blocks = lax.axis_size("blk")
    lines = rows // LANES
    dma = pltpu.SemaphoreType.DMA
    vmem = pl.BlockSpec(memory_space=pltpu.VMEM)
    hbm = pl.BlockSpec(memory_space=pltpu.HBM)
    f32, i32, bf16 = jnp.float32, jnp.int32, jnp.bfloat16
    early, late = pl.pallas_call(
        functools.partial(kernel, blocks, copies),
        out_shape=[jax.ShapeDtypeStruct((1, rows), f32)] * 2,
        in_specs=[hbm, hbm],
        out_specs=[vmem, vmem],
        scratch_shapes=[
            pltpu.VMEM((rows, width), f32),
            pltpu.VMEM((3, 2 * copies * lines, LANES), i32),
            pltpu.VMEM((9, rows, width), bf16),
            pltpu.VMEM((rows, width), bf16),
            pltpu.VMEM((rows // 2, width), bf16),
            pltpu.VMEM((2, rows, LANES), i32),
            pltpu.VMEM((rows, LANES), i32),
            pltpu.VMEM((rows // 2, LANES), i32),
            pltpu.VMEM((2, rows, LANES), f32),
            pltpu.VMEM((rows, LANES), f32),
            pltpu.VMEM((rows // 2, LANES), f32),
            pltpu.VMEM((8, 8, rows), f32),
            pltpu.VMEM((4, 8, rows), f32),
            pltpu.VMEM((7, 2, rows), f32),
            pltpu.VMEM((7, 2, rows), f32),
            pltpu.VMEM((2, 2, rows), f32),
            pltpu.VMEM((2, 2, rows), f32),
            pltpu.VMEM((2, rows // 2), f32),
            pltpu.VMEM((2, 2, rows // 2), f32),
            dma((CHUNKS,)), dma,
            dma, dma, dma, dma((CHUNKS,)), dma, dma((CHUNKS,)), dma, dma((2,)), dma((2 * CHUNKS,)),
            dma, dma, dma((CHUNKS,)), dma((3,)), dma((3, 2)), dma, dma,
            dma, dma, dma((2,)), dma((2,)), dma, dma,
        ],
        compiler_params=pltpu.CompilerParams(
            collective_id=0, has_side_effects=True, vmem_limit_bytes=56_500_000
        ),
    )(embeddings, ranks.reshape(-1, LANES))
    return early.reshape(rows), late.reshape(rows)


def solution(mesh):
    return jax.shard_map(
        shards,
        mesh=mesh,
        in_specs=(P(("blk", "rep"), None), P()),
        out_specs=(P(("blk", "rep")), P(("blk", "rep"))),
        check_vma=False,
    )
```

time: 62.9 us -> 44.6 us (0.71)
  the two profiles are of different devices: /device:TPU:0 before, /device:TPU:8 now
where the time goes in v2:
time: 44.6 us; the launch traced here: 44.4 us
  Pallas kernels  42.6 us (96%)
  local copies, waits for them, and re-layouts  1.16 us (3%)
  between operations  0.64 us (1%)
    pallas_call x1, Pallas kernels, shards(): pl.pallas_call(functools.partial(kernel, blocks, copies), out_shape=[jax....  42.6 us
    unnamed x2, local copies, waits for them, and re-layouts  1.16 us

profile of v2, /device:TPU:8, one launch (start us, length us, event | category | flops | bytes accessed | tf_op | source)
XLA Modules:
  0.0 44.4 jit_solution(6273074623816791562)
XLA Ops:
  0.6 42.6 %shard_map.41 = (f32[1,512]{1,0:T(1,128)S(1)}, f32[1,512]{1,0:T(1,128)S(1)}) custom-call(f32[512,768]{1,0:T(8,128)} %emb_hbm.1, s32[128,128]{1,0:T(8,128)} %bitcast.5), custom_call_target="tpu_custom_call" | custom-call | tf_op jit(solution)/shard_map/pallas_call | solution.py:512
  43.3 0.6 %copy.6 = f32[512]{0:T(512)} copy(f32[512]{0:T(512)S(1)} %bitcast.4) | data formatting | bytes 4096
  43.9 0.6 %copy.7 = f32[512]{0:T(512)} copy(f32[512]{0:T(512)S(1)} %bitcast.3) | data formatting | bytes 4096

commit v3 on v2

--- a/solution.py
+++ b/solution.py
@@ -13,7 +13,7 @@
 
 
 def kernel(
-    blocks, copies, emb_hbm, ranks_hbm, early_ref, late_ref,
+    blocks, copies, emb_hbm, ranks_hbm, out_ref,
     emb, rank, mem, pair, two,
     guest_rank, pair_rank, two_rank, guest_acc, pair_acc, two_acc, host_acc, swap_acc,
     row_out, row_in, back_out, back_in, two_out, two_in,
@@ -23,6 +23,7 @@
     row_send, row_sem, back_send, back_recv, twob_send, twob_recv,
 ):
     rows = emb.shape[0]
+    early_ref, late_ref = out_ref.at[0:1], out_ref.at[1:2]
     part = rows // CHUNKS
     unit = rows // 2
     small = part // 2
@@ -57,10 +58,12 @@
         last = l // (layers - 1)
         is_relay = l == 1
         has_two = lax.rem(l, 2) == 0
+        two_turn = l // 2
     else:
         last = 0 * l
         is_relay = None
         has_two = None
+        two_turn = 0 * l
 
     def if_relay(f):
         if wrap:
@@ -136,7 +139,7 @@
         return mem.at[h + 1]
 
     def area(u):
-        return pl.ds(u * unit, unit)
+        return pl.ds(pl.multiple_of(u * unit, unit), unit)
 
     every = pl.ds(0, rows)
 
@@ -273,7 +276,7 @@
                 kept = jnp.where(line < own, scores[:, at], jnp.float32(-1.0))
                 best = jnp.maximum(best, kept)
                 column = jnp.max(kept.reshape(count // 8, 8, LANES), axis=0)
-                there = slice(low + g * LANES, low + (g + 1) * LANES)
+                there = pl.ds(pl.multiple_of(low + g * LANES, LANES), LANES)
                 acc[slot + k, :, there] = jnp.maximum(acc[slot + k, :, there], column)
         best_ref[...] = best.reshape(best_ref.shape)
 
@@ -318,14 +321,23 @@
     with jax.named_scope("own1"):
         own_score(1)
 
-    def arrive(p):
+    def arrive(p, u):
         for by_x in (True, False):
             i = 2 * p + (0 if by_x else 1)
-            u = i // half
 
             @if_relay
             def _():
                 relay(i)
+                if u == 1:
+                    k = i - half
+
+                    @pl.when(k < 4 - 2 * x)
+                    def _():
+                        own_score(2 + k, 0)
+
+                    @pl.when(k < 2)
+                    def _():
+                        part_score(0, k)
 
             with jax.named_scope("y"):
                 y_copy(i).wait_recv()
@@ -335,43 +347,59 @@
             twin_copy(1, u, cut(i)).start()
             diag_copy(i, by_x).start()
 
+    def two_post(u):
+        @if_two
+        def _():
+            @pl.when(two_turn == u)
+            def _():
+                two_copy(0, unit).start()
+
     def z_wait(u):
         with jax.named_scope("z"):
             z_copy(u, area(u)).wait_recv()
 
     for u in range(2):
-        each(arrive, u * (half // 2), (u + 1) * (half // 2))
+        each(lambda p: arrive(p, u), u * (half // 2), (u + 1) * (half // 2))
         with jax.named_scope("twin"):
             for k in range(2):
                 twin_copy(k, u, area(u)).wait_recv()
 
-        @unless_relay
-        def _():
-            with jax.named_scope("own25"):
-                sweep(lambda h: own_score(h, u), 2, 6 - 2 * x)
-            if u == 0:
+        if u == 0:
+            two_post(0)
+
+            @unless_relay
+            def _():
+                with jax.named_scope("own25"):
+                    sweep(lambda h: own_score(h, 0), 2, 6 - 2 * x)
                 z_wait(0)
                 with jax.named_scope("v0"):
                     sweep(lambda h: part_score(0, h), 0, 2)
-            else:
-                with jax.named_scope("v0"):
-                    sweep(lambda h: part_score(0, h), 2, 6)
-
-                @if_two
-                def _():
-                    two_copy(0, unit).start()
-                z_wait(1)
-                with jax.named_scope("v1"):
-                    sweep(lambda h: part_score(1, h), 0, 6)
-
-    @if_relay
-    def _():
-        with jax.named_scope("own25"):
-            sweep(own_score, 2, 6 - 2 * x)
-        z_wait(0)
-        z_wait(1)
-        with jax.named_scope("v01"):
-            sweep(up_score, 0, 6)
+
+            @if_relay
+            def _():
+                z_wait(0)
+
+    def diag_arrive(i):
+        diag_copy(i, True).wait_recv()
+        twin_copy(2, i // half, cut(i)).start()
+
+    with jax.named_scope("own25"):
+        sweep(lambda h: own_score(h, 1), 2, 6 - 2 * x)
+    with jax.named_scope("v0"):
+        sweep(lambda h: part_score(0, h), 2, 2 + 2 * x)
+        two_post(1)
+        sweep(lambda h: part_score(0, h), 2 + 2 * x, 6)
+    z_wait(1)
+
+    def later(h):
+        @pl.when(h == 3)
+        def _():
+            with jax.named_scope("diag"):
+                each(diag_arrive, 0, half)
+        part_score(1, h)
+
+    with jax.named_scope("v1"):
+        sweep(later, 0, 6)
 
     def lanes(acc):
         return jnp.max(acc[...].T, axis=0, keepdims=True)
@@ -381,28 +409,35 @@
     def back_copy(slot):
         target = far_up if slot else device(layer(-1), x, r)
         return send(back_out.at[slot], back_in.at[slot], back_send.at[slot], back_recv.at[slot], target)
-
-    def diag_arrive(i):
-        diag_copy(i, True).wait_recv()
-        twin_copy(2, i // half, cut(i)).start()
 
     @if_relay
     def _():
         with jax.named_scope("p45"):
             sweep(pair_score, 4, 6)
 
-    for u in range(2):
-        with jax.named_scope("diag"):
-            each(diag_arrive, u * half, (u + 1) * half)
-            twin_copy(2, u, area(u)).wait_recv()
-        with jax.named_scope("last"):
-            @pl.when(x == 0)
-            def _():
-                sweep(lambda h: both_score(h, u), 6, 8)
-
-            @pl.when(x == 1)
-            def _():
-                sweep(lambda h: up_score(h, u), 6, 8)
+    def last_score(t):
+        u, odd = t // 2, lax.rem(t, 2)
+
+        @pl.when(t == 2)
+        def _():
+            with jax.named_scope("diag"):
+                each(diag_arrive, half, CHUNKS)
+
+        @pl.when(odd == 1)
+        def _():
+            with jax.named_scope("twin2"):
+                twin_copy(2, u, area(u)).wait_recv()
+
+        @pl.when(x == 0)
+        def _():
+            both_score(6 + odd, u)
+
+        @pl.when(x == 1)
+        def _():
+            up_score(6 + odd, u)
+
+    with jax.named_scope("last"):
+        each(last_score, 0, 4)
 
     back_out[0, 0:1, :] = none
     back_out[0, 1:2, :] = lanes(guest_acc.at[0])
@@ -417,6 +452,30 @@
             back_out[1, 1:2, :] = jnp.where(x == 0, none, best)
             back_copy(1).start()
 
+    def row_copy(h):
+        return send(row_out.at[h - 1], row_in.at[h - 1], row_send, row_sem, peer(h))
+
+    def row_post(h):
+        row_out[h - 1, 0:1, :] = jnp.max(host_acc[h], axis=0, keepdims=True)
+        row_out[h - 1, 1:2, :] = none
+        row_copy(h).start()
+
+    @unless_relay
+    def _():
+        sweep(row_post, 4 - 3 * x, 8 - 4 * x)
+
+    def row_merge(h):
+        best = jnp.max(host_acc[h], axis=0, keepdims=True)
+        swapped = jnp.max(swap_acc[h - 4], axis=0, keepdims=True)
+        row_out[h - 1, 0:1, :] = jnp.where(x == 0, best, jnp.maximum(best, swapped))
+        row_out[h - 1, 1:2, :] = jnp.where(x == 0, swapped, none)
+        row_copy(h).start()
+
+    @if_relay
+    def _():
+        sweep(row_merge, 4, 8)
+        sweep(row_post, 1, 4)
+
     @if_two
     def _():
         with jax.named_scope("two"):
@@ -424,20 +483,10 @@
         with jax.named_scope("v2"):
             sweep(lambda k: two_score(4 * x + 2 * k), 0, 2)
 
-    def row_copy(h):
-        return send(row_out.at[h - 1], row_in.at[h - 1], row_send, row_sem, peer(h))
-
     with jax.named_scope("rows"):
-        for h in range(7, 0, -1):
-            best = jnp.max(host_acc[h], axis=0, keepdims=True)
-            other = none
-            if h >= 4 and wrap:
-                swapped = jnp.max(swap_acc[h - 4], axis=0, keepdims=True)
-                other = jnp.where(x == 0, swapped, none)
-                best = jnp.where(x == 0, best, jnp.maximum(best, swapped))
-            row_out[h - 1, 0:1, :] = best
-            row_out[h - 1, 1:2, :] = other
-            row_copy(h).start()
+        @unless_relay
+        def _():
+            sweep(row_post, 1 + 3 * x, 4 + 4 * x)
 
     def twob_copy(k):
         return send(two_out, two_in.at[k], twob_send, twob_recv, device(layer(-2), 1, r))
@@ -509,11 +558,11 @@
     vmem = pl.BlockSpec(memory_space=pltpu.VMEM)
     hbm = pl.BlockSpec(memory_space=pltpu.HBM)
     f32, i32, bf16 = jnp.float32, jnp.int32, jnp.bfloat16
-    early, late = pl.pallas_call(
+    both = pl.pallas_call(
         functools.partial(kernel, blocks, copies),
-        out_shape=[jax.ShapeDtypeStruct((1, rows), f32)] * 2,
+        out_shape=jax.ShapeDtypeStruct((2, rows), f32),
         in_specs=[hbm, hbm],
-        out_specs=[vmem, vmem],
+        out_specs=vmem,
         scratch_shapes=[
             pltpu.VMEM((rows, width), f32),
             pltpu.VMEM((3, 2 * copies * lines, LANES), i32),
@@ -543,7 +592,7 @@
             collective_id=0, has_side_effects=True, vmem_limit_bytes=56_500_000
         ),
     )(embeddings, ranks.reshape(-1, LANES))
-    return early.reshape(rows), late.reshape(rows)
+    return both[0], both[1]
 
 
 def solution(mesh):

time: 44.6 us -> 42.4 us (0.951)
  Pallas kernels: 42.6 us -> 41 us
  local copies, waits for them, and re-layouts: 1.16 us -> 0.59 us
    pallas_call x1, Pallas kernels: 42.6 us -> 41 us  [shards(): pl.pallas_call(functools.partial(kernel, blocks, copies), out_shape=jax.S...]
    unnamed x2 -> x0, local copies, waits for them, and re-layouts: 1.16 us -> none
    slice x0 -> x1, local copies, waits for them, and re-layouts: none -> 0.59 us  [shards(): return (both[0], both[1])]
where the time goes in v3:
time: 42.4 us; the launch traced here: 42.3 us
  Pallas kernels  41 us (97%)
  between operations  0.64 us (2%)
  local copies, waits for them, and re-layouts  0.59 us (1%)
    pallas_call x1, Pallas kernels, shards(): pl.pallas_call(functools.partial(kernel, blocks, copies), out_shape=jax.S...  41 us

profile of v3, /device:TPU:8, one launch (start us, length us, event | category | flops | bytes accessed | tf_op | source)
XLA Modules:
  0.0 42.3 jit_solution(12992908653906654017)
XLA Ops:
  0.6 41.0 %shard_map.41 = f32[2,512]{1,0:T(2,128)S(1)} custom-call(f32[512,768]{1,0:T(8,128)} %emb_hbm.1, s32[128,128]{1,0:T(8,128)} %bitcast.3), custom_call_target="tpu_custom_call" | custom-call | tf_op jit(solution)/shard_map/pallas_call | solution.py:561
  41.7 0.6 %fusion = (f32[1,512]{1,0:T(1,128)}, f32[1,512]{1,0:T(1,128)}) fusion(f32[2,512]{1,0:T(2,128)S(1)} %shard_map.41), kind=kLoop, calls=%fused_computation | loop fusion | bytes 8192 | tf_op jit(solution)/shard_map/slice | solution.py:595

commit v4 on v3

--- a/solution.py
+++ b/solution.py
@@ -12,7 +12,7 @@
 MESH = pl.DeviceIdType.MESH
 
 
-def kernel(
+def program(
     blocks, copies, emb_hbm, ranks_hbm, out_ref,
     emb, rank, mem, pair, two,
     guest_rank, pair_rank, two_rank, guest_acc, pair_acc, two_acc, host_acc, swap_acc,
@@ -297,7 +297,7 @@
         score(pair, pair_rank, pair_acc, h, None, swap_acc, h - 4, sign)
 
     def two_score(h):
-        score(two, two_rank, two_acc, h, None, host_acc, h, slots=2)
+        score(two, two_rank, two_acc, h, None, host_acc, h, slots=4)
 
     def sweep(f, low, high):
         def body(h, _):
@@ -384,18 +384,19 @@
         twin_copy(2, i // half, cut(i)).start()
 
     with jax.named_scope("own25"):
-        sweep(lambda h: own_score(h, 1), 2, 6 - 2 * x)
+        sweep(lambda h: own_score(h, 1), 2, 5 - x)
+        two_post(1)
+        sweep(lambda h: own_score(h, 1), 5 - x, 6 - 2 * x)
     with jax.named_scope("v0"):
-        sweep(lambda h: part_score(0, h), 2, 2 + 2 * x)
-        two_post(1)
-        sweep(lambda h: part_score(0, h), 2 + 2 * x, 6)
+        sweep(lambda h: part_score(0, h), 2, 6)
     z_wait(1)
 
     def later(h):
-        @pl.when(h == 3)
-        def _():
-            with jax.named_scope("diag"):
-                each(diag_arrive, 0, half)
+        for turn, low in ((0, 0), (2, 2), (5, half)):
+            @pl.when(h == turn)
+            def _():
+                with jax.named_scope("diag"):
+                    each(diag_arrive, low, low + 2)
         part_score(1, h)
 
     with jax.named_scope("v1"):
@@ -410,47 +411,48 @@
         target = far_up if slot else device(layer(-1), x, r)
         return send(back_out.at[slot], back_in.at[slot], back_send.at[slot], back_recv.at[slot], target)
 
+    def last_score(t):
+        u, odd = t // 2, lax.rem(t, 2)
+
+        @pl.when(t == 1)
+        def _():
+            with jax.named_scope("diag"):
+                each(diag_arrive, half + 2, CHUNKS)
+
+        @pl.when(odd == 1)
+        def _():
+            with jax.named_scope("twin2"):
+                twin_copy(2, u, area(u)).wait_recv()
+
+        @pl.when(x == 0)
+        def _():
+            both_score(6 + odd, u)
+
+        @pl.when(x == 1)
+        def _():
+            up_score(6 + odd, u)
+
+        @if_relay
+        def _():
+            with jax.named_scope("pair"):
+                pair_score(4 + t)
+
+    with jax.named_scope("last"):
+        each(last_score, 0, 4)
+
     @if_relay
     def _():
-        with jax.named_scope("p45"):
-            sweep(pair_score, 4, 6)
-
-    def last_score(t):
-        u, odd = t // 2, lax.rem(t, 2)
-
-        @pl.when(t == 2)
-        def _():
-            with jax.named_scope("diag"):
-                each(diag_arrive, half, CHUNKS)
-
-        @pl.when(odd == 1)
-        def _():
-            with jax.named_scope("twin2"):
-                twin_copy(2, u, area(u)).wait_recv()
-
-        @pl.when(x == 0)
-        def _():
-            both_score(6 + odd, u)
-
-        @pl.when(x == 1)
-        def _():
-            up_score(6 + odd, u)
-
-    with jax.named_scope("last"):
-        each(last_score, 0, 4)
+        best = lanes(pair_acc)
+        back_out[1, 0:1, :] = jnp.where(x == 0, best, none)
+        back_out[1, 1:2, :] = jnp.where(x == 0, none, best)
+        back_copy(1).start()
 
     back_out[0, 0:1, :] = none
     back_out[0, 1:2, :] = lanes(guest_acc.at[0])
     back_copy(0).start()
 
-    @if_relay
-    def _():
-        with jax.named_scope("p67"):
-            sweep(pair_score, 6, 8)
-            best = lanes(pair_acc)
-            back_out[1, 0:1, :] = jnp.where(x == 0, best, none)
-            back_out[1, 1:2, :] = jnp.where(x == 0, none, best)
-            back_copy(1).start()
+    def twob_copy(k):
+        return send(two_out, two_in.at[k], twob_send, twob_recv, device(layer(-2), 1, r))
 
     def row_copy(h):
         return send(row_out.at[h - 1], row_in.at[h - 1], row_send, row_sem, peer(h))
@@ -481,20 +483,14 @@
         with jax.named_scope("two"):
             two_copy(0, unit).wait_recv()
         with jax.named_scope("v2"):
-            sweep(lambda k: two_score(4 * x + 2 * k), 0, 2)
+            two_score(4 * x)
+        two_out[...] = jnp.broadcast_to(lanes(two_acc), two_out.shape)
+        twob_copy(x).start()
 
     with jax.named_scope("rows"):
         @unless_relay
         def _():
             sweep(row_post, 1 + 3 * x, 4 + 4 * x)
-
-    def twob_copy(k):
-        return send(two_out, two_in.at[k], twob_send, twob_recv, device(layer(-2), 1, r))
-
-    @if_two
-    def _():
-        two_out[...] = jnp.broadcast_to(lanes(two_acc), two_out.shape)
-        twob_copy(x).start()
 
     late_ref[...] = jnp.max(host_acc[0], axis=0, keepdims=True)
     early_ref[...] = lanes(guest_acc.at[1])
@@ -549,12 +545,22 @@
             back_copy(1).wait_send()
 
 
+def kernel(blocks, copies, *refs):
+    dma = pltpu.SemaphoreType.DMA
+    pl.run_scoped(
+        functools.partial(program, blocks, copies, *refs),
+        dma((CHUNKS,)), dma,
+        dma, dma, dma, dma((CHUNKS,)), dma, dma((CHUNKS,)), dma, dma((2,)), dma((2 * CHUNKS,)),
+        dma, dma, dma((CHUNKS,)), dma((3,)), dma((3, 2)), dma, dma,
+        dma, dma, dma((2,)), dma((2,)), dma, dma,
+    )
+
+
 def shards(embeddings, ranks):
     rows, width = embeddings.shape
     copies = lax.axis_size("rep")
     blocks = lax.axis_size("blk")
     lines = rows // LANES
-    dma = pltpu.SemaphoreType.DMA
     vmem = pl.BlockSpec(memory_space=pltpu.VMEM)
     hbm = pl.BlockSpec(memory_space=pltpu.HBM)
     f32, i32, bf16 = jnp.float32, jnp.int32, jnp.bfloat16
@@ -583,10 +589,6 @@
             pltpu.VMEM((2, 2, rows), f32),
             pltpu.VMEM((2, rows // 2), f32),
             pltpu.VMEM((2, 2, rows // 2), f32),
-            dma((CHUNKS,)), dma,
-            dma, dma, dma, dma((CHUNKS,)), dma, dma((CHUNKS,)), dma, dma((2,)), dma((2 * CHUNKS,)),
-            dma, dma, dma((CHUNKS,)), dma((3,)), dma((3, 2)), dma, dma,
-            dma, dma, dma((2,)), dma((2,)), dma, dma,
         ],
         compiler_params=pltpu.CompilerParams(
             collective_id=0, has_side_effects=True, vmem_limit_bytes=56_500_000

time: 42.4 us -> 41 us (0.967)
  Pallas kernels: 41 us -> 39.6 us
    pallas_call x1, Pallas kernels: 41 us -> 39.6 us  [shards(): pl.pallas_call(functools.partial(kernel, blocks, copies), out_shape=jax.S...]
where the time goes in v4:
time: 41 us; the launch traced here: 40.8 us
  Pallas kernels  39.6 us (97%)
  between operations  0.64 us (2%)
  local copies, waits for them, and re-layouts  0.59 us (1%)
    pallas_call x1, Pallas kernels, shards(): pl.pallas_call(functools.partial(kernel, blocks, copies), out_shape=jax.S...  39.6 us

profile of v4, /device:TPU:8, one launch (start us, length us, event | category | flops | bytes accessed | tf_op | source)
XLA Modules:
  0.0 40.8 jit_solution(8400548159777826813)
XLA Ops:
  0.6 39.6 %shard_map.41 = f32[2,512]{1,0:T(2,128)S(1)} custom-call(f32[512,768]{1,0:T(8,128)} %refs_0_.1, s32[128,128]{1,0:T(8,128)} %bitcast.3), custom_call_target="tpu_custom_call" | custom-call | tf_op jit(solution)/shard_map/pallas_call | solution.py:567
  40.2 0.6 %fusion = (f32[1,512]{1,0:T(1,128)}, f32[1,512]{1,0:T(1,128)}) fusion(f32[2,512]{1,0:T(2,128)S(1)} %shard_map.41), kind=kLoop, calls=%fused_computation | loop fusion | bytes 8192 | tf_op jit(solution)/shard_map/slice | solution.py:597

commit v5 on v4

--- a/solution.py
+++ b/solution.py
@@ -20,7 +20,7 @@
     emb_sem, rank_sem,
     core_send, core_recv, x_send, x_recv, y_send, y_recv, z_send, z_recv, pair_recv,
     relay_send, diag_send, diag_recv, twin_send, twin_recv, two_send, two_recv,
-    row_send, row_sem, back_send, back_recv, twob_send, twob_recv,
+    row_send, row_sem, back_send, back_recv, twob_send, twob_recv, drained,
 ):
     rows = emb.shape[0]
     early_ref, late_ref = out_ref.at[0:1], out_ref.at[1:2]
@@ -83,8 +83,12 @@
 
     up = device(layer(1), x, r)
     down = device(layer(-1), x, r)
+    cross = flip_rep(1)
     far_up = device(layer(2), x, r)
     far_down = device(layer(-2), x, r)
+    cross_up = device(layer(2), x, cross)
+    cross_down = device(layer(-2), x, cross)
+    relay_to = device(layer(-1), x, cross)
 
     def cut(i):
         return pl.ds(pl.multiple_of(i * part, part), part)
@@ -109,15 +113,20 @@
     if wrap:
         @pl.when(l == 0)
         def _():
-            greet(device(l + 1, x, r))
+            greet(device(l + 1, x, cross))
 
         @pl.when(l > 0)
         def _():
             greet(down)
 
-        @pl.when(l < layers - 1)
+        @pl.when(is_relay)
+        def _():
+            greet(cross_up)
+
+        @pl.when(has_two)
         def _():
             greet(far_up)
+
         expected = 5 - last
     else:
         greet(down)
@@ -158,10 +167,10 @@
         return send(host(0).at[at], mem.at[0, at], z_send, z_recv.at[u], up)
 
     def far_copy(k, at):
-        return send(host(0).at[at], pair.at[at], z_send, pair_recv.at[k], far_down)
+        return send(host(0).at[at], pair.at[at], z_send, pair_recv.at[k], cross_down)
 
     def relay_copy(u, at):
-        return send(pair.at[at], mem.at[0, at], relay_send, z_recv.at[u], down)
+        return send(pair.at[at], mem.at[0, at], relay_send, z_recv.at[u], relay_to)
 
     def diag_copy(i, by_x, at=None):
         at = cut(i) if at is None else at
@@ -235,6 +244,10 @@
             with jax.named_scope("w"):
                 far_copy(k, piece(k)).wait_recv()
             relay_copy(i // half, piece(k)).start()
+
+        @pl.when(i == CHUNKS - 1)
+        def _():
+            pl.semaphore_signal(drained, inc=1, device_id=up, device_id_type=MESH)
 
     sign = 2 * x - 1
 
@@ -294,7 +307,7 @@
         score(mem.at[0, at], guest_rank.at[0, at], guest_acc.at[0, at], h, u, host_acc, h)
 
     def pair_score(h):
-        score(pair, pair_rank, pair_acc, h, None, swap_acc, h - 4, sign)
+        score(pair, pair_rank, pair_acc, h, None, swap_acc, h - 4, sign, slots=2)
 
     def two_score(h):
         score(two, two_rank, two_acc, h, None, host_acc, h, slots=4)
@@ -314,7 +327,7 @@
     with jax.named_scope("own0"):
         own_score(0)
     spread(1, place(x, r), lines, guest_rank.at[0])
-    spread(2, place(x, r), lines, pair_rank, sign)
+    spread(2, place(x, cross), lines, pair_rank, sign)
     spread(2, place(1, r) + x * (lines // 2), lines // 2, two_rank)
     with jax.named_scope("core"):
         core_copy(every).wait_recv()
@@ -383,24 +396,57 @@
         diag_copy(i, True).wait_recv()
         twin_copy(2, i // half, cut(i)).start()
 
-    with jax.named_scope("own25"):
-        sweep(lambda h: own_score(h, 1), 2, 5 - x)
-        two_post(1)
-        sweep(lambda h: own_score(h, 1), 5 - x, 6 - 2 * x)
-    with jax.named_scope("v0"):
-        sweep(lambda h: part_score(0, h), 2, 6)
-    z_wait(1)
-
-    def later(h):
-        for turn, low in ((0, 0), (2, 2), (5, half)):
-            @pl.when(h == turn)
-            def _():
-                with jax.named_scope("diag"):
-                    each(diag_arrive, low, low + 2)
-        part_score(1, h)
-
-    with jax.named_scope("v1"):
-        sweep(later, 0, 6)
+    def wait_drained():
+        @if_two
+        def _():
+            @pl.when(two_turn == 1)
+            def _():
+                with jax.named_scope("drained"):
+                    pl.semaphore_wait(drained, 1)
+
+    def diag_pair(low):
+        with jax.named_scope("diag"):
+            each(diag_arrive, low, low + 2)
+
+    def steady():
+        if wrap:
+            wait_drained()
+        z_wait(1)
+        with jax.named_scope("both"):
+            sweep(lambda h: both_score(h, 1), 2, 2)
+            two_post(1)
+            sweep(lambda h: both_score(h, 1), 2, 6 - 2 * x)
+            sweep(lambda h: up_score(h, 1), 6 - 2 * x, 6)
+        diag_pair(0)
+        with jax.named_scope("up"):
+            sweep(lambda h: up_score(h, 0), 2, 6)
+        diag_pair(2)
+        with jax.named_scope("v1"):
+            sweep(lambda h: part_score(1, h), 0, 2)
+
+    def delayed():
+        with jax.named_scope("own25"):
+            sweep(lambda h: own_score(h, 1), 2, 6 - 2 * x)
+        with jax.named_scope("v0"):
+            sweep(lambda h: part_score(0, h), 2, 6)
+        diag_pair(0)
+        z_wait(1)
+
+        def later(h):
+            @pl.when(h == 2)
+            def _():
+                diag_pair(2)
+            part_score(1, h)
+
+        with jax.named_scope("v1"):
+            sweep(later, 0, 6)
+
+    if wrap:
+        pl.when(l > 0)(steady)
+        pl.when(l == 0)(delayed)
+    else:
+        steady()
+    diag_pair(half)
 
     def lanes(acc):
         return jnp.max(acc[...].T, axis=0, keepdims=True)
@@ -408,16 +454,15 @@
     none = jnp.full((1, rows), -1.0, jnp.float32)
 
     def back_copy(slot):
-        target = far_up if slot else device(layer(-1), x, r)
+        target = cross_up if slot else device(layer(-1), x, r)
         return send(back_out.at[slot], back_in.at[slot], back_send.at[slot], back_recv.at[slot], target)
 
     def last_score(t):
         u, odd = t // 2, lax.rem(t, 2)
 
-        @pl.when(t == 1)
-        def _():
-            with jax.named_scope("diag"):
-                each(diag_arrive, half + 2, CHUNKS)
+        @pl.when(t == 2)
+        def _():
+            diag_pair(half + 2)
 
         @pl.when(odd == 1)
         def _():
@@ -434,8 +479,10 @@
 
         @if_relay
         def _():
-            with jax.named_scope("pair"):
-                pair_score(4 + t)
+            @pl.when(odd == u)
+            def _():
+                with jax.named_scope("pair"):
+                    pair_score(4 + t - odd)
 
     with jax.named_scope("last"):
         each(last_score, 0, 4)
@@ -552,7 +599,7 @@
         dma((CHUNKS,)), dma,
         dma, dma, dma, dma((CHUNKS,)), dma, dma((CHUNKS,)), dma, dma((2,)), dma((2 * CHUNKS,)),
         dma, dma, dma((CHUNKS,)), dma((3,)), dma((3, 2)), dma, dma,
-        dma, dma, dma((2,)), dma((2,)), dma, dma,
+        dma, dma, dma((2,)), dma((2,)), dma, dma, pltpu.SemaphoreType.REGULAR,
     )
 
 

time: 41 us -> 40.3 us (0.983); the launches traced: 40.8 us -> 39.6 us
  Pallas kernels: 39.6 us -> 38.4 us
    pallas_call x1, Pallas kernels: 39.6 us -> 38.4 us  [shards(): pl.pallas_call(functools.partial(kernel, blocks, copies), out_shape=jax.S...]
where the time goes in v5:
time: 40.3 us; the launch traced here: 39.6 us
  Pallas kernels  38.4 us (95%)
  between operations  0.64 us (2%)
  local copies, waits for them, and re-layouts  0.59 us (1%)
    pallas_call x1, Pallas kernels, shards(): pl.pallas_call(functools.partial(kernel, blocks, copies), out_shape=jax.S...  38.4 us

profile of v5, /device:TPU:8, one launch (start us, length us, event | category | flops | bytes accessed | tf_op | source)
XLA Modules:
  0.0 39.6 jit_solution(15895440830068656829)
XLA Ops:
  0.6 38.4 %shard_map.41 = f32[2,512]{1,0:T(2,128)S(1)} custom-call(f32[512,768]{1,0:T(8,128)} %refs_0_.1, s32[128,128]{1,0:T(8,128)} %bitcast.3), custom_call_target="tpu_custom_call" | custom-call | tf_op jit(solution)/shard_map/pallas_call | solution.py:614
  39.0 0.6 %fusion = (f32[1,512]{1,0:T(1,128)}, f32[1,512]{1,0:T(1,128)}) fusion(f32[2,512]{1,0:T(2,128)S(1)} %shard_map.41), kind=kLoop, calls=%fused_computation | loop fusion | bytes 8192 | tf_op jit(solution)/shard_map/slice | solution.py:644

commit v6 on v5

--- a/solution.py
+++ b/solution.py
@@ -27,6 +27,7 @@
     part = rows // CHUNKS
     unit = rows // 2
     small = part // 2
+    head = part + small
     half = CHUNKS // 2
     lines = rows // LANES
     layers = blocks // 2
@@ -184,8 +185,8 @@
         )
 
     def two_copy(i, size):
-        at = pl.ds(pl.multiple_of(x * unit + i * part, part), size)
-        there = pl.ds(i * part, size)
+        at = pl.ds(pl.multiple_of(x * unit + i, small), size)
+        there = pl.ds(i, size)
         return send(host(4 * (1 - x)).at[at], two.at[there], two_send, two_recv, far_up)
 
     def normalise(i):
@@ -245,9 +246,6 @@
                 far_copy(k, piece(k)).wait_recv()
             relay_copy(i // half, piece(k)).start()
 
-        @pl.when(i == CHUNKS - 1)
-        def _():
-            pl.semaphore_signal(drained, inc=1, device_id=up, device_id_type=MESH)
 
     sign = 2 * x - 1
 
@@ -360,12 +358,12 @@
             twin_copy(1, u, cut(i)).start()
             diag_copy(i, by_x).start()
 
-    def two_post(u):
+    def two_post(turn, low, size):
         @if_two
         def _():
-            @pl.when(two_turn == u)
-            def _():
-                two_copy(0, unit).start()
+            @pl.when(two_turn == turn)
+            def _():
+                two_copy(low, size).start()
 
     def z_wait(u):
         with jax.named_scope("z"):
@@ -378,7 +376,7 @@
                 twin_copy(k, u, area(u)).wait_recv()
 
         if u == 0:
-            two_post(0)
+            two_post(0, 0, unit)
 
             @unless_relay
             def _():
@@ -396,26 +394,32 @@
         diag_copy(i, True).wait_recv()
         twin_copy(2, i // half, cut(i)).start()
 
-    def wait_drained():
-        @if_two
-        def _():
-            @pl.when(two_turn == 1)
-            def _():
-                with jax.named_scope("drained"):
-                    pl.semaphore_wait(drained, 1)
+    def hand_over():
+        @if_relay
+        def _():
+            with jax.named_scope("relayed"):
+                relay_copy(0, every).wait_send()
+            pl.semaphore_signal(drained, inc=1, device_id=up, device_id_type=MESH)
+
+        @pl.when(l == 2)
+        def _():
+            with jax.named_scope("drained"):
+                pl.semaphore_wait(drained, 1)
+            two_copy(head, unit - head).start()
 
     def diag_pair(low):
         with jax.named_scope("diag"):
             each(diag_arrive, low, low + 2)
 
     def steady():
+        z_wait(1)
         if wrap:
-            wait_drained()
-        z_wait(1)
+            two_post(1, 0, head)
         with jax.named_scope("both"):
-            sweep(lambda h: both_score(h, 1), 2, 2)
-            two_post(1)
-            sweep(lambda h: both_score(h, 1), 2, 6 - 2 * x)
+            sweep(lambda h: both_score(h, 1), 2, 3)
+            if wrap:
+                hand_over()
+            sweep(lambda h: both_score(h, 1), 3, 6 - 2 * x)
             sweep(lambda h: up_score(h, 1), 6 - 2 * x, 6)
         diag_pair(0)
         with jax.named_scope("up"):
@@ -588,7 +592,6 @@
 
         @if_relay
         def _():
-            relay_copy(0, every).wait_send()
             back_copy(1).wait_send()
 
 

time: 40.3 us -> 39.7 us (0.985); the launches traced: 39.6 us -> 39.6 us
  no operation moved by 1% of the time
where the time goes in v6:
time: 39.7 us; the launch traced here: 39.6 us
  Pallas kernels  38.4 us (97%)
  between operations  0.64 us (2%)
  local copies, waits for them, and re-layouts  0.59 us (1%)
    pallas_call x1, Pallas kernels, shards(): pl.pallas_call(functools.partial(kernel, blocks, copies), out_shape=jax.S...  38.4 us

profile of v6, /device:TPU:8, one launch (start us, length us, event | category | flops | bytes accessed | tf_op | source)
XLA Modules:
  0.0 39.6 jit_solution(3804551736710799313)
XLA Ops:
  0.6 38.4 %shard_map.41 = f32[2,512]{1,0:T(2,128)S(1)} custom-call(f32[512,768]{1,0:T(8,128)} %refs_0_.1, s32[128,128]{1,0:T(8,128)} %bitcast.3), custom_call_target="tpu_custom_call" | custom-call | tf_op jit(solution)/shard_map/pallas_call | solution.py:617
  39.0 0.6 %fusion = (f32[1,512]{1,0:T(1,128)}, f32[1,512]{1,0:T(1,128)}) fusion(f32[2,512]{1,0:T(2,128)S(1)} %shard_map.41), kind=kLoop, calls=%fused_computation | loop fusion | bytes 8192 | tf_op jit(solution)/shard_map/slice | solution.py:647

commit v7 on v6

--- a/solution.py
+++ b/solution.py
@@ -104,6 +104,9 @@
             rank.at[k], rank_sem,
         )
 
+    emb_copy(0).start()
+    emb_copy(1).start()
+
     barrier = pltpu.get_barrier_semaphore()
 
     def greet(target):
@@ -134,7 +137,7 @@
         greet(far_down)
         expected = 5
 
-    for i in range(CHUNKS):
+    for i in range(2, CHUNKS):
         emb_copy(i).start()
     for k in range(3):
         rank_copy(k).start()

time: 39.7 us -> 39.7 us (level)
  no operation moved by 1% of the time
where the time goes in v7:
time: 39.7 us; the launch traced here: 39.6 us
  Pallas kernels  38.4 us (97%)
  between operations  0.64 us (2%)
  local copies, waits for them, and re-layouts  0.59 us (1%)
    pallas_call x1, Pallas kernels, shards(): pl.pallas_call(functools.partial(kernel, blocks, copies), out_shape=jax.S...  38.4 us

profile of v7, /device:TPU:8, one launch (start us, length us, event | category | flops | bytes accessed | tf_op | source)
XLA Modules:
  0.0 39.6 jit_solution(17508630559672111382)
XLA Ops:
  0.6 38.4 %shard_map.41 = f32[2,512]{1,0:T(2,128)S(1)} custom-call(f32[512,768]{1,0:T(8,128)} %refs_0_.1, s32[128,128]{1,0:T(8,128)} %bitcast.3), custom_call_target="tpu_custom_call" | custom-call | tf_op jit(solution)/shard_map/pallas_call | solution.py:620
  39.0 0.6 %fusion = (f32[1,512]{1,0:T(1,128)}, f32[1,512]{1,0:T(1,128)}) fusion(f32[2,512]{1,0:T(2,128)S(1)} %shard_map.41), kind=kLoop, calls=%fused_computation | loop fusion | bytes 8192 | tf_op jit(solution)/shard_map/slice | solution.py:650
